TPU v7x, 32 devices: a whole 2x2x4 slice. The times are simulated.
32 devices in a mesh: rep: 1, r: 8 (over y, z), s: 4 (over x, core).
Axes of the slice: x: 2, y: 2, z: 4, core: 2. Of those that a mesh axis runs over, the one named last changes fastest.
Arguments:
- x: bfloat16 [32, 4096, 640], P(('rep', 'r', 's'))
- dy: bfloat16 [32, 4096, 640], P(('rep', 'r', 's'))
- w_gate: bfloat16 [2, 640, 2048], P(None, 's')
- w_up: bfloat16 [2, 640, 2048], P(None, 's')
- w_down: bfloat16 [2, 2048, 640], P(None, 's')
- m_w_gate: float32 [2, 640, 2048], P(None, 's')
- m_w_up: float32 [2, 640, 2048], P(None, 's')
- m_w_down: float32 [2, 2048, 640], P(None, 's')
- v_w_gate: float32 [2, 640, 2048], P(None, 's')
- v_w_up: float32 [2, 640, 2048], P(None, 's')
- v_w_down: float32 [2, 2048, 640], P(None, 's')
Outputs:
- output 1: bfloat16 [2, 640, 2048], P('rep', 's')
- output 2: bfloat16 [2, 640, 2048], P('rep', 's')
- output 3: bfloat16 [2, 2048, 640], P('rep', 's')
- output 4: float32 [2, 640, 2048], P('rep', 's')
- output 5: float32 [2, 640, 2048], P('rep', 's')
- output 6: float32 [2, 2048, 640], P('rep', 's')
- output 7: float32 [2, 640, 2048], P('rep', 's')
- output 8: float32 [2, 640, 2048], P('rep', 's')
- output 9: float32 [2, 2048, 640], P('rep', 's')
All inputs are finite; a program needn't handle non-finite values.
Results may differ from a plain program's by a relative error of at most 0.022.
Values are sent between devices in bfloat16 or wider.
A program may use at most 2 GiB of HBM per device.

v0:
```python
import jax
import jax.numpy as jnp
from jax import lax
from jax.sharding import PartitionSpec as P

NAMES = ("w_gate", "w_up", "w_down")


def matmul(a, w):
    return jnp.dot(a, w, preferred_element_type=jnp.float32).astype(jnp.bfloat16)


def normed(h):
    wide = h.astype(jnp.float32)
    scale = lax.rsqrt(jnp.mean(wide**2, -1, keepdims=True) + 1e-6)
    return (wide * scale).astype(jnp.bfloat16)


def layer(h, w):
    a = normed(h)
    gate = jnp.dot(a, w["w_gate"], preferred_element_type=jnp.float32)
    up = jnp.dot(a, w["w_up"], preferred_element_type=jnp.float32)
    return h + matmul((jax.nn.silu(gate) * up).astype(jnp.bfloat16), w["w_down"])


def adamw(w, m, v, g):
    m = 0.9 * m + 0.1 * g
    v = 0.95 * v + 0.05 * g * g
    step = m * lax.rsqrt(v + 1e-8) + 0.1 * w
    return (w - 0.02 * step).astype(jnp.bfloat16), m, v


def solution(mesh):
    def fetched(weights, number):
        return {name: lax.all_gather(w[number], "s", axis=0, tiled=True) for name, w in zip(NAMES, weights, strict=True)}

    def summed(term):
        return lax.psum(lax.psum_scatter(term, "s", scatter_dimension=0, tiled=True), "r")

    def step(x, dy, *arrays):
        weights, m, v = (arrays[i : i + 3] for i in (0, 3, 6))
        layers = weights[0].shape[0]
        h, kept = x[0], []
        for number in range(layers):
            kept.append(h)
            h = layer(h, fetched(weights, number))
        by_h, mine = dy[0], [None] * layers
        for number in reversed(range(layers)):
            _, back = jax.vjp(lambda w, h: layer(h, w), fetched(weights, number), kept[number])
            by_w, by_h = back(by_h)
            mine[number] = [summed(by_w[name]) for name in NAMES]
        gradients = [jnp.stack([mine[number][i] for number in range(layers)]).astype(jnp.float32) for i in range(3)]
        new = [adamw(w.astype(jnp.float32), m, v, g) for w, m, v, g in zip(weights, m, v, gradients, strict=True)]
        return tuple(one[which] for which in range(3) for one in new)

    states, cut = P(("rep", "r", "s"), None, None), P(None, "s", None)
    return jax.shard_map(
        step,
        mesh=mesh,
        in_specs=(states, states) + (cut,) * 9,
        out_specs=(P("rep", "s", None),) * 9,
        check_vma=False,
    )
```

profile of v0, /device:TPU:0, one launch (start us, length us, event | category | flops | bytes accessed | tf_op | source)
XLA Modules:
  0.0 691.4 jit_solution(5957176050365973902)
XLA Ops:
  7.2 0.0 all-gather.13.cloned.1.call-start
  7.2 2.6 fusion.97
  9.8 0.0 all-gather.13.cloned.1.call-update
  9.8 0.0 all-gather.15.cloned.1.call-start
  9.9 2.5 fusion.96
  12.4 0.0 all-gather.15.cloned.1.call-update
  12.4 0.0 all-gather.17.cloned.1.call-start
  12.5 1.2 fusion.95
  13.6 0.0 all-gather.17.cloned.1.call-update
  13.7 0.0 all-gather.21.cloned.1.call-start
  13.7 0.5 all-gather.21.cloned.1.call-update
  14.2 0.0 all-gather.23.cloned.1.call-start
  14.3 0.5 all-gather.23.cloned.1.call-update
  14.8 0.0 all-gather.19.cloned.1.call-start
  14.9 0.5 all-gather.19.cloned.1.call-update
  15.4 0.0 reduce-scatter.15.cloned.1.call-start
  15.4 7.9 %copy.20 = bf16[1,4096,640]{1,2,0:T(8,128)(2,1)} copy(bf16[1,4096,640]{2,1,0:T(8,128)(2,1)} %param.11) | data formatting | bytes 10485760 | tf_op args[0]
  23.4 3.6 fusion.15
  27.0 7.9 %copy.21 = bf16[1,4096,640]{1,2,0:T(8,128)(2,1)} copy(bf16[1,4096,640]{2,1,0:T(8,128)(2,1)} %param.12) | data formatting | bytes 10485760 | tf_op args[1]
  34.9 3.2 all-gather.13.cloned.1.call-done
  38.1 21.8 %fusion.40 = f32[4096,2048]{1,0:T(8,128)} fusion(bf16[1,4096,640]{1,2,0:T(8,128)(2,1)} %copy.20, f32[4096]{0:T(1024)S(1)} %add_rsqrt_fusion, bf16[1,640,2048]{2,1,0:T(8,128)(2,1)} %all-gather.13.cloned.1.call-done), kind=kOutput, calls=%fused_computation.55 | convolution fusion | flops 10745282560 | bytes 41435136 | tf_op jit(solution)/shard_map/dot_general | solution.py:21
  59.9 5.6 all-gather.15.cloned.1.call-done
  65.5 34.0 %multiply_convert_fusion.1 = (bf16[4096,2048]{1,0:T(8,128)(2,1)}, f32[4096,2048]{1,0:T(8,128)}) fusion(f32[4096,2048]{1,0:T(8,128)} %fusion.40, bf16[1,640,2048]{2,1,0:T(8,128)(2,1)} %all-gather.15.cloned.1.call-done, bf16[1,4096,640]{1,2,0:T(8,128)(2,1)} %copy.20, f32[4096]{0:T(1024)S(1)} %add_rsqrt_fusion), kind=kOutput, calls=%fused_computation.17 | convolution fusion | flops 10795614208 | bytes 91766784 | tf_op jit(solution)/shard_map/dot_general | solution.py:22
  99.5 18.7 %fusion.19 = (f32[4096]{0:T(1024)S(1)}, bf16[4096,640]{0,1:T(8,128)(2,1)}) fusion(bf16[4096,2048]{1,0:T(8,128)(2,1)} %get-tuple-element.30, bf16[1,2048,640]{2,1,0:T(8,128)(2,1)} %all-gather.17.cloned.1.call-done, bf16[1,4096,640]{1,2,0:T(8,128)(2,1)} %copy.20), kind=kOutput, calls=%fused_computation.37 | convolution fusion | flops 10750521344 | bytes 29900800 | tf_op jit(solution)/shard_map/dot_general | solution.py:10
  118.2 1.9 all-gather.21.cloned.1.call-done
  120.1 19.9 %convolution_convert_fusion.1 = bf16[4096,2048]{1,0:T(8,128)(2,1)} fusion(bf16[1,4096,640]{2,1,0:T(8,128)(2,1)} %param.12, bf16[1,2048,640]{2,1,0:T(8,128)(2,1)} %all-gather.21.cloned.1.call-done), kind=kOutput, calls=%fused_computation.29 | convolution fusion | flops 10745806848 | bytes 24641536 | tf_op jit(solution)/shard_map/transpose(jvp())/dot_general | solution.py:10
  140.0 7.3 %all-gather.23.cloned.1.call-done = bf16[1,640,2048]{2,1,0:T(8,128)(2,1)} async-done(((bf16[1,160,2048]{2,1,0:T(8,128)(2,1)}), bf16[1,640,2048]{2,1,0:T(8,128)(2,1)}) %all-gather.23.cloned.1.call-update) | async-done | bytes 2621456 | tf_op jit(solution)/shard_map/all_gather | solution.py:35
  147.3 21.8 %fusion.32 = f32[4096,2048]{1,0:T(8,128)} fusion(bf16[4096,640]{0,1:T(8,128)(2,1)} %get-tuple-element.33, f32[4096]{0:T(1024)S(1)} %fusion.83, bf16[1,640,2048]{2,1,0:T(8,128)(2,1)} %all-gather.23.cloned.1.call-done), kind=kOutput, calls=%fused_computation.52 | convolution fusion | flops 10745282560 | bytes 41435136 | tf_op jit(solution)/shard_map/jvp()/dot_general | solution.py:22
  169.1 5.5 all-gather.19.cloned.1.call-done
  174.6 44.8 %fusion.2 = (bf16[4096,2048]{1,0:T(8,128)(2,1)}, f32[4096,2048]{1,0:T(8,128)}) fusion(f32[4096,2048]{1,0:T(8,128)} %fusion.32, bf16[4096,2048]{1,0:T(8,128)(2,1)} %convolution_convert_fusion.1, bf16[1,640,2048]{2,1,0:T(8,128)(2,1)} %all-gather.19.cloned.1.call-done, bf16[4096,640]{0,1:T(8,128)(2,1)} %get-tuple-element.33, f32[4096]{0:T(1024)S(1)} %fusion.83), kind=kOutput, calls=%fused_computation.8 | convolution fusion | flops 10845945856 | bytes 108544000 | tf_op jit(solution)/shard_map/jvp()/dot_general | solution.py:21
  219.4 17.1 %convolution_convert_fusion.3 = bf16[4096,640]{0,1:T(8,128)(2,1)} fusion(bf16[4096,2048]{1,0:T(8,128)(2,1)} %get-tuple-element.34, bf16[1,640,2048]{2,1,0:T(8,128)(2,1)} %all-gather.19.cloned.1.call-done), kind=kOutput, calls=%fused_computation.42 | convolution fusion | flops 10737418240 | bytes 24641536 | tf_op jit(solution)/shard_map/transpose(jvp())/dot_general | solution.py:21
  236.5 25.5 %fusion.21 = (f32[4096]{0:T(1024)S(1)}, bf16[4096,640]{0,1:T(8,128)(2,1)}) fusion(bf16[4096,640]{0,1:T(8,128)(2,1)} %get-tuple-element.33, bf16[4096,640]{0,1:T(8,128)(2,1)} %convolution_convert_fusion.3, bf16[1,640,2048]{2,1,0:T(8,128)(2,1)S(1)} %copy-done.17, bf16[4096,2048]{1,0:T(8,128)(2,1)} %convolution_convert_fusion.1, ...), kind=kOutput, calls=%fused_computation.39 | convolution fusion | flops 10803474432 | bytes 68698112 | tf_op jit(solution)/shard_map/transpose(jvp())/dot_general | solution.py:22
  262.0 11.9 %fusion.26 = bf16[4096,640]{0,1:T(8,128)(2,1)} fusion(bf16[4096,640]{0,1:T(8,128)(2,1)} %get-tuple-element.33, bf16[4096,640]{0,1:T(8,128)(2,1)} %get-tuple-element.37, bf16[1,4096,640]{1,2,0:T(8,128)(2,1)} %copy.21, f32[4096]{0:T(1024)S(1)} %multiply_multiply_fusion.3, f32[4096]{0:T(1024)S(1)} %fusion.83), kind=kLoop, calls=%fused_computation.45 | loop fusion | flops 18350080 | bytes 21004288 | tf_op jit(solution)/shard_map/transpose(jvp())/add_any | solution.py:14
  273.9 19.6 %convolution_convert_fusion.4 = bf16[2048,640]{1,0:T(8,128)(2,1)} fusion(bf16[4096,2048]{1,0:T(8,128)(2,1)} %get-tuple-element.30, bf16[4096,640]{0,1:T(8,128)(2,1)} %fusion.26), kind=kOutput, calls=%fused_computation.68 | convolution fusion | flops 10738728960 | bytes 24641536 | tf_op jit(solution)/shard_map/transpose(jvp())/dot_general | solution.py:10
  293.5 0.0 reduce-scatter.15.cloned.1.call-update
  293.5 0.0 reduce-scatter.17.cloned.1.call-start
  293.6 27.2 %fusion.45 = bf16[2048,640]{1,0:T(8,128)(2,1)} fusion(bf16[1,4096,640]{2,1,0:T(8,128)(2,1)} %param.12, f32[4096,2048]{1,0:T(8,128)} %fusion.32, f32[4096,2048]{1,0:T(8,128)} %get-tuple-element.35), kind=kOutput, calls=%fused_computation.66 | convolution fusion | flops 10789060608 | bytes 74973184 | tf_op jit(solution)/shard_map/transpose(jvp())/dot_general | solution.py:10
  320.8 0.0 reduce-scatter.17.cloned.1.call-update
  320.8 0.0 reduce-scatter.11.cloned.1.call-start
  320.9 18.8 %convolution_convert_fusion = bf16[4096,2048]{1,0:T(8,128)(2,1)} fusion(bf16[4096,640]{0,1:T(8,128)(2,1)} %fusion.26, bf16[1,2048,640]{2,1,0:T(8,128)(2,1)S(1)} %copy-done.16), kind=kOutput, calls=%fused_computation.28 | convolution fusion | flops 10745806848 | bytes 24641536 | tf_op jit(solution)/shard_map/transpose(jvp())/dot_general | solution.py:10
  339.7 22.4 %fusion.56 = bf16[640,2048]{1,0:T(8,128)(2,1)} fusion(bf16[4096,2048]{1,0:T(8,128)(2,1)} %convolution_convert_fusion, f32[4096,2048]{1,0:T(8,128)} %fusion.40, bf16[1,4096,640]{1,2,0:T(8,128)(2,1)} %copy.20, f32[4096]{0:T(1024)S(1)} %copy-done.15), kind=kOutput, calls=%fused_computation.70 | convolution fusion | flops 10796924928 | bytes 58212352 | tf_op jit(solution)/shard_map/transpose(jvp())/dot_general | solution.py:22
  362.1 0.0 reduce-scatter.13.cloned.1.call-start
  362.2 22.4 %fusion.48 = bf16[640,2048]{1,0:T(8,128)(2,1)} fusion(bf16[4096,2048]{1,0:T(8,128)(2,1)} %convolution_convert_fusion.1, bf16[4096,640]{0,1:T(8,128)(2,1)} %get-tuple-element.33, f32[4096]{0:T(1024)S(1)} %copy-done.11, f32[4096,2048]{1,0:T(8,128)} %get-tuple-element.35), kind=kOutput, calls=%fused_computation.67 | convolution fusion | flops 10796924928 | bytes 58212352 | tf_op jit(solution)/shard_map/transpose(jvp())/dot_general | solution.py:22
  384.6 0.0 reduce-scatter.13.cloned.1.call-update
  384.6 0.0 reduce-scatter.7.cloned.1.call-start
  384.6 35.4 %fusion.51 = bf16[640,2048]{1,0:T(8,128)(2,1)} fusion(f32[4096,2048]{1,0:T(8,128)} %fusion.40, f32[4096,2048]{1,0:T(8,128)} %get-tuple-element.31, bf16[4096,2048]{1,0:T(8,128)(2,1)} %convolution_convert_fusion, bf16[1,4096,640]{1,2,0:T(8,128)(2,1)} %copy.20, f32[4096]{0:T(1024)S(1)} %copy-done.15), kind=kOutput, calls=%fused_computation.69 | convolution fusion | flops 10838867968 | bytes 91766784 | tf_op jit(solution)/shard_map/transpose(jvp())/dot_general | solution.py:21
  420.0 0.0 reduce-scatter.7.cloned.1.call-update
  420.0 0.0 reduce-scatter.9.cloned.1.call-start
  420.1 17.1 %fusion.42 = bf16[640,2048]{1,0:T(8,128)(2,1)} fusion(bf16[4096,2048]{1,0:T(8,128)(2,1)} %get-tuple-element.34, bf16[4096,640]{0,1:T(8,128)(2,1)} %get-tuple-element.33, f32[4096]{0:T(1024)S(1)} %copy-done.11), kind=kOutput, calls=%fused_computation.65 | convolution fusion | flops 10745282560 | bytes 24657920 | tf_op jit(solution)/shard_map/transpose(jvp())/dot_general | solution.py:21
  437.2 0.0 all-reduce.3.cloned.1.call-start
  437.2 0.0 reduce-scatter.15.cloned.1.call-done
  437.3 0.0 reduce-scatter.17.cloned.1.call-done
  437.3 0.0 reduce-scatter.11.cloned.1.call-done
  437.3 2.8 reduce-scatter.13.cloned.1.call-done
  440.1 37.4 %reduce-scatter.7.cloned.1.call-done = bf16[160,2048]{1,0:T(8,128)(2,1)} async-done(((bf16[640,2048]{1,0:T(8,128)(2,1)}), bf16[160,2048]{1,0:T(8,128)(2,1)}) %reduce-scatter.7.cloned.1.call-update) | async-done | bytes 655376 | tf_op jit(solution)/shard_map/reduce_scatter | solution.py:38
  477.5 37.3 %reduce-scatter.9.cloned.1.call-done = bf16[160,2048]{1,0:T(8,128)(2,1)} async-done(((bf16[640,2048]{1,0:T(8,128)(2,1)}), bf16[160,2048]{1,0:T(8,128)(2,1)}) %reduce-scatter.9.cloned.1.call-update) | async-done | bytes 655376 | tf_op jit(solution)/shard_map/reduce_scatter | solution.py:38
  514.8 0.0 all-reduce.3.cloned.1.call-update
  514.8 152.9 %all-reduce.3.cloned.1.call-done = (bf16[1,160,2048]{2,1,0:T(8,128)(2,1)}, bf16[1,160,2048]{2,1,0:T(8,128)(2,1)}, bf16[1,160,2048]{2,1,0:T(8,128)(2,1)}, bf16[1,...) async-done(((bf16[1,160,2048]{2,1,0:T(8,128)(2,1)}, bf16[1,160,2048]{2,1,0:T(8,128)(2,1)}, bf16[1,160,2048]{2,1,0:T(8,128)(2,1)}, ...) | async-done | bytes 3932176 | tf_op jit(solution)/shard_map/psum | solution.py:38
  667.8 6.9 fusion.69
  674.7 1.4 copy-done.6
  676.1 0.7 copy-done.7
  676.8 0.1 copy-done.8
  676.9 0.2 copy-done.9
  677.1 7.3 %fusion.61 = (bf16[2,160,2048]{2,1,0:T(8,128)(2,1)}, f32[2,160,2048]{2,1,0:T(8,128)}, f32[2,160,2048]{2,1,0:T(8,128)}, bf16[2,160,2048]{2,1,0:T(8,128)(2,1)}, f3...) fusion(bf16[2,160,2048]{2,1,0:T(8,128)(2,1)S(1)} %copy-done, bf16[1,160,2048]{2,1,0:T(8,128)(2,1)S(1)} %copy-done.8, ...), kind=kLoop, calls=%fused_computation.73 | loop fusion | flops 24903680 | bytes 28835840 | tf_op jit(solution)/shard_map/convert_element_type | solution.py:30
  (38 shorter events, 0.1 us)
Async XLA Ops:
  7.2 5.3 copy-start.2
  7.2 30.9 %all-gather.13.cloned.1.call-start = ((), (), s32[]{:S(2)}) async-start(), calls=%async_computation.12 | async-start | bytes 3276800 | tf_op jit(solution)/shard_map/all_gather | solution.py:35
  9.8 55.7 %all-gather.15.cloned.1.call-start = ((), (), s32[]{:S(2)}) async-start(), calls=%async_computation.13 | async-start | bytes 3276800 | tf_op jit(solution)/shard_map/all_gather | solution.py:35
  12.4 87.1 %all-gather.17.cloned.1.call-start = ((), (), s32[]{:S(2)}) async-start(), calls=%async_computation.14 | async-start | bytes 3276800 | tf_op jit(solution)/shard_map/all_gather | solution.py:35
  13.7 106.5 %all-gather.21.cloned.1.call-start = ((), (), s32[]{:S(2)}) async-start(), calls=%async_computation.16 | async-start | bytes 3276800 | tf_op jit(solution)/shard_map/all_gather | solution.py:35
  14.2 133.1 %all-gather.23.cloned.1.call-start = ((), (), s32[]{:S(2)}) async-start(), calls=%async_computation.17 | async-start | bytes 3276800 | tf_op jit(solution)/shard_map/all_gather | solution.py:35
  14.8 159.7 %all-gather.19.cloned.1.call-start = ((), (), s32[]{:S(2)}) async-start(), calls=%async_computation.15 | async-start | bytes 3276800 | tf_op jit(solution)/shard_map/all_gather | solution.py:35
  15.4 421.9 %reduce-scatter.15.cloned.1.call-start = ((), (), s32[]{:S(2)}) async-start(), calls=%async_computation.10 | async-start | bytes 3276800 | tf_op jit(solution)/shard_map/reduce_scatter | solution.py:38
  27.0 38.5 %copy-start.14 = (f32[4096]{0:T(1024)}, f32[4096]{0:T(1024)S(1)}, u32[]{:S(2)}) copy-start(f32[4096]{0:T(1024)S(1)} %add_rsqrt_fusion) | copy-start | bytes 49156
  118.1 21.8 %copy-start.12 = (f32[4096]{0:T(1024)}, f32[4096]{0:T(1024)S(1)}, u32[]{:S(2)}) copy-start(f32[4096]{0:T(1024)S(1)} %get-tuple-element.32) | copy-start | bytes 49156
  118.1 143.9 %copy-start.10 = (f32[4096]{0:T(1024)}, f32[4096]{0:T(1024)S(1)}, u32[]{:S(2)}) copy-start(f32[4096]{0:T(1024)S(1)} %fusion.83) | copy-start | bytes 49156
  219.4 17.1 %copy-start.17 = (bf16[1,640,2048]{2,1,0:T(8,128)(2,1)S(1)}, bf16[1,640,2048]{2,1,0:T(8,128)(2,1)}, u32[]{:S(2)}) copy-start(bf16[1,640,2048]{2,1,0:T(8,128)(2,1)} %all-gather.23.cloned.1.call-done) | copy-start | bytes 7864324
  236.5 25.5 %copy-start.13 = (f32[4096]{0:T(1024)S(1)}, f32[4096]{0:T(1024)}, u32[]{:S(2)}) copy-start(f32[4096]{0:T(1024)} %copy-done.12) | copy-start | bytes 49156
  293.5 27.3 %copy-start.16 = (bf16[1,2048,640]{2,1,0:T(8,128)(2,1)S(1)}, bf16[1,2048,640]{2,1,0:T(8,128)(2,1)}, u32[]{:S(2)}) copy-start(bf16[1,2048,640]{2,1,0:T(8,128)(2,1)} %all-gather.17.cloned.1.call-done) | copy-start | bytes 7864324
  293.5 143.7 %reduce-scatter.17.cloned.1.call-start = ((), (), s32[]{:S(2)}) async-start(), calls=%async_computation.11 | async-start | bytes 3276800 | tf_op jit(solution)/shard_map/reduce_scatter | solution.py:38
  320.8 18.9 %copy-start.15 = (f32[4096]{0:T(1024)S(1)}, f32[4096]{0:T(1024)}, u32[]{:S(2)}) copy-start(f32[4096]{0:T(1024)} %copy-done.14) | copy-start | bytes 49156
  320.8 116.5 %reduce-scatter.11.cloned.1.call-start = ((), (), s32[]{:S(2)}) async-start(), calls=%async_computation.8 | async-start | bytes 3276800 | tf_op jit(solution)/shard_map/reduce_scatter | solution.py:38
  339.7 22.5 %copy-start.11 = (f32[4096]{0:T(1024)S(1)}, f32[4096]{0:T(1024)}, u32[]{:S(2)}) copy-start(f32[4096]{0:T(1024)} %copy-done.10) | copy-start | bytes 49156
  362.1 78.0 %reduce-scatter.13.cloned.1.call-start = ((), (), s32[]{:S(2)}) async-start(), calls=%async_computation.9 | async-start | bytes 3276800 | tf_op jit(solution)/shard_map/reduce_scatter | solution.py:38
  384.6 92.9 %reduce-scatter.7.cloned.1.call-start = ((), (), s32[]{:S(2)}) async-start(), calls=%async_computation.6 | async-start | bytes 3276800 | tf_op jit(solution)/shard_map/reduce_scatter | solution.py:38
  420.0 94.8 %reduce-scatter.9.cloned.1.call-start = ((), (), s32[]{:S(2)}) async-start(), calls=%async_computation.7 | async-start | bytes 3276800 | tf_op jit(solution)/shard_map/reduce_scatter | solution.py:38
  437.2 230.6 %copy-start.3 = (bf16[2,512,640]{2,1,0:T(8,128)(2,1)S(1)}, bf16[2,512,640]{2,1,0:T(8,128)(2,1)}, u32[]{:S(2)}) copy-start(bf16[2,512,640]{2,1,0:T(8,128)(2,1)} %param.15) | copy-start | bytes 3932164
  437.2 230.5 %all-reduce.3.cloned.1.call-start = ((), (), s32[]{:S(2)}) async-start(), calls=%async_computation.18 | async-start | bytes 7864320 | tf_op jit(solution)/shard_map/psum | solution.py:38
  667.7 6.9 %copy-start = (bf16[2,160,2048]{2,1,0:T(8,128)(2,1)S(1)}, bf16[2,160,2048]{2,1,0:T(8,128)(2,1)}, u32[]{:S(2)}) copy-start(bf16[2,160,2048]{2,1,0:T(8,128)(2,1)} %param.13) | copy-start | bytes 3932164
  667.7 6.9 %copy-start.1 = (bf16[2,160,2048]{2,1,0:T(8,128)(2,1)S(1)}, bf16[2,160,2048]{2,1,0:T(8,128)(2,1)}, u32[]{:S(2)}) copy-start(bf16[2,160,2048]{2,1,0:T(8,128)(2,1)} %param.14) | copy-start | bytes 3932164
  667.7 6.9 %copy-start.4 = (f32[2,160,2048]{2,1,0:T(8,128)S(1)}, f32[2,160,2048]{2,1,0:T(8,128)}, u32[]{:S(2)}) copy-start(f32[2,160,2048]{2,1,0:T(8,128)} %param.19) | copy-start | bytes 7864324
  667.7 6.9 %copy-start.5 = (f32[2,160,2048]{2,1,0:T(8,128)S(1)}, f32[2,160,2048]{2,1,0:T(8,128)}, u32[]{:S(2)}) copy-start(f32[2,160,2048]{2,1,0:T(8,128)} %param.16) | copy-start | bytes 7864324
  667.7 8.3 %copy-start.6 = (f32[2,160,2048]{2,1,0:T(8,128)S(1)}, f32[2,160,2048]{2,1,0:T(8,128)}, u32[]{:S(2)}) copy-start(f32[2,160,2048]{2,1,0:T(8,128)} %param.20) | copy-start | bytes 7864324
  667.8 9.1 %copy-start.7 = (f32[2,160,2048]{2,1,0:T(8,128)S(1)}, f32[2,160,2048]{2,1,0:T(8,128)}, u32[]{:S(2)}) copy-start(f32[2,160,2048]{2,1,0:T(8,128)} %param.17) | copy-start | bytes 7864324
  667.8 9.1 %copy-start.8 = (bf16[1,160,2048]{2,1,0:T(8,128)(2,1)S(1)}, bf16[1,160,2048]{2,1,0:T(8,128)(2,1)}, u32[]{:S(2)}) copy-start(bf16[1,160,2048]{2,1,0:T(8,128)(2,1)} %get-tuple-element.9) | copy-start | bytes 1966084
  667.8 9.3 %copy-start.9 = (bf16[1,160,2048]{2,1,0:T(8,128)(2,1)S(1)}, bf16[1,160,2048]{2,1,0:T(8,128)(2,1)}, u32[]{:S(2)}) copy-start(bf16[1,160,2048]{2,1,0:T(8,128)(2,1)} %get-tuple-element.10) | copy-start | bytes 1966084
Sparse Core Ops, SparseCore 0:
  10.1 27.9 all-gather.12
  40.3 25.1 all-gather.14
  67.6 25.1 all-gather.16
  94.9 25.1 all-gather.20
  122.1 25.1 all-gather.22
  149.3 25.1 all-gather.18
  293.7 34.2 reduce-scatter.14
  331.1 34.2 reduce-scatter.16
  368.5 34.2 reduce-scatter.10
  405.8 34.2 reduce-scatter.12
  443.2 34.2 reduce-scatter.6
  480.5 34.2 reduce-scatter.8
  519.1 148.6 all-reduce.2
where the time goes:
time: 698 us; the launch traced here: 691 us
  matrix products  366 us (52%)
  waiting for transfers between devices  256 us (37%)
  other arithmetic  29.7 us (4%)
  local copies, waits for them, and re-layouts  24.6 us (4%)
  between operations  14.5 us (2%)
    psum x1, waiting for transfers between devices, summed(): lax.psum(lax.psum_scatter(term, 's', scatter_dimension=0, tiled=True), 'r')  153 us
    dot_general x5, matrix products, layer(): gate = jnp.dot(a, w['w_gate'], preferred_element_type=jnp.float32)  136 us
    dot_general x5, matrix products, layer(): up = jnp.dot(a, w['w_up'], preferred_element_type=jnp.float32)  126 us
    dot_general x5, matrix products, matmul(): jnp.dot(a, w, preferred_element_type=jnp.float32).astype(jnp.bfloat16)  104 us
    reduce_scatter x6, waiting for transfers between devices, summed(): lax.psum_scatter(term, 's', scatter_dimension=0, tiled=True)  77.5 us
    all_gather x6, waiting for transfers between devices, fetched(): lax.all_gather(w[number], 's', axis=0, tiled=True)  23.5 us
    unnamed x38, local copies, waits for them, and re-layouts  18.3 us
    convert_element_type x2, other arithmetic, adamw(): return ((w - 0.02 * step).astype(jnp.bfloat16), m, v)  14.2 us
  transfers between devices with their start and end apart: 13, of which 9 were waited for; matrix products, arithmetic and copies ran while one was open for 41% of the time, Pallas kernels for 0%

commit v1 on v0

v1 whole, which is shorter than its diff:
```python
import functools

import jax
import jax.numpy as jnp
from jax import lax
from jax.experimental import pallas as pl
from jax.experimental.pallas import tpu as pltpu
from jax.sharding import PartitionSpec as P

MESH = pl.DeviceIdType.MESH
f32, bf16 = jnp.float32, jnp.bfloat16
N, D, FF, L = 4096, 640, 2048, 2
F = 512
J = FF // F
T = 1024
NT = N // T
ROWS, COLS = D // 4, F // 4
NN, TN, TT = (((1,), (0,)), ((), ())), (((0,), (0,)), ((), ())), (((1,), (1,)), ((), ()))


def dot(a, b, dims=NN):
    return lax.dot_general(a, b, dims, preferred_element_type=f32)


def of(start, size, by=8):
    return pl.ds(pl.multiple_of(start, by), size)


def normed(h):
    wide = h.astype(f32)
    return (wide * lax.rsqrt(jnp.mean(wide * wide, -1, keepdims=True) + 1e-6)).astype(bf16)


def step_kernel(
    x_h, dy_h, wg_h, wu_h, wd_h,
    ggu_h, gd_h, h1_h, a0_h, grad_h,
    a, g, act, acc, wgu, wd, stg, rc, xs, rx, ys, ry, accy, zs, rz, fin,
    gs_sem, gr_sem, w_sem, t_sem, o_sem, out_sem,
    cs, cr, xss, xrs, yss, yrs, zss, zrs, ass_, ars, bss, brs,
):
    s, r = lax.axis_index("s"), lax.axis_index("r")
    xx, core = s // 2, s % 2
    y, z = r // 4, r % 4
    sib, xn = {"s": 2 * xx + 1 - core}, {"s": 2 * (1 - xx) + core}
    yn = {"r": 4 * (1 - y) + z}
    zn = {k: {"r": 4 * y + (z + k) % 4} for k in (1, 2, 3)}

    def remote(src, dst, ss, rs, to):
        return pltpu.make_async_remote_copy(src_ref=src, dst_ref=dst, send_sem=ss, recv_sem=rs, device_id=to, device_id_type=MESH)

    barrier = pltpu.get_barrier_semaphore()
    for peer in (sib, xn, yn, zn[1], zn[2], zn[3]):
        pl.semaphore_signal(barrier, inc=1, device_id=peer, device_id_type=MESH)

    def tile(t):
        return of(t * T, T, T)

    def load_x(t):
        return pltpu.make_async_copy(x_h.at[tile(t)], g.at[tile(t)], t_sem.at[t])

    def keep_a0(t):
        return pltpu.make_async_copy(a.at[tile(t)], a0_h.at[tile(t)], o_sem.at[t])

    for t in range(NT):
        load_x(t).start()
    pl.semaphore_wait(barrier, 6)

    def part_gu(u, owner, h=None):
        cols = pl.ds(0, F) if h is None else of(256 * h, 256, 256)
        return ggu_h.at[u, :, of(owner * ROWS, ROWS, ROWS), cols]

    def part_d(u, owner, h=None):
        rows = of(owner * COLS, COLS, COLS) if h is None else of(owner * COLS + 64 * h, 64, 64)
        return gd_h.at[u, rows]

    def own_pieces(u, blocks):
        layer, j = u // J, u % J
        for which, w in enumerate((wg_h, wu_h)):
            for b in blocks:
                yield w.at[layer, :, of(b * F + j * COLS, COLS, COLS)], which, of(b * COLS, COLS, COLS)

    def own_d(u, h=None):
        layer, j = u // J, u % J
        rows = of(j * COLS, COLS, COLS) if h is None else of(j * COLS + 64 * h, 64, 64)
        return wd_h.at[layer, rows]

    def send_own(u):
        for h, path, to in ((y, 1, xn), (None, 0, sib)):
            blocks = range(4) if h is None else (2 * h, 2 * h + 1)
            for src, which, cols in own_pieces(u, blocks):
                remote(src, ggu_h.at[u, which, of(s * ROWS, ROWS, ROWS), cols], gs_sem.at[u, path, 0], gr_sem.at[u, path, 0], to).start()
            remote(own_d(u, h), part_d(u, s, h), gs_sem.at[u, path, 1], gr_sem.at[u, path, 1], to).start()

    def gather_copy(u, path, which, half=None):
        owner = {0: s, 1: s, 2: xn["s"], 3: xn["s"], 4: xn["s"]}[path]
        h = {0: None, 1: y, 2: y, 3: y, 4: 1 - y}[path]
        to = {0: sib, 1: xn, 2: yn, 3: sib, 4: sib}[path]
        ref = (part_gu, part_d)[which](u, owner, h)
        return remote(ref, ref, gs_sem.at[u, path, which], gr_sem.at[u, path, which], to)

    def forward_x(u, which):
        gather_copy(u, 1, which).wait_recv()
        gather_copy(u, 2, which).start()
        gather_copy(u, 3, which).start()

    def forward_y(u, which):
        gather_copy(u, 2, which).wait_recv()
        gather_copy(u, 4, which).start()

    def both(fn, u):
        fn(u, 0)
        fn(u, 1)

    def arrived(u, which):
        for path in (0, 3, 4):
            gather_copy(u, path, which).wait_recv()

    def load_gu(u, slot):
        for src, which, cols in own_pieces(u, range(4)):
            pltpu.make_async_copy(src, wgu.at[slot, which, of(s * ROWS, ROWS, ROWS), cols], w_sem.at[slot, 0]).start()
        for k in (1, 2, 3):
            owner = (s + k) % 4
            pltpu.make_async_copy(part_gu(u, owner), wgu.at[slot, :, of(owner * ROWS, ROWS, ROWS)], w_sem.at[slot, 0]).start()

    def load_d(u, slot):
        pltpu.make_async_copy(own_d(u), wd.at[slot, of(s * COLS, COLS, COLS)], w_sem.at[slot, 1]).start()
        for k in (1, 2, 3):
            owner = (s + k) % 4
            pltpu.make_async_copy(part_d(u, owner), wd.at[slot, of(owner * COLS, COLS, COLS)], w_sem.at[slot, 1]).start()

    def loaded(slot, which):
        ref = (wgu, wd)[which].at[slot]
        pltpu.make_async_copy(ref, ref, w_sem.at[slot, which]).wait()

    for u in range(2 * J):
        send_own(u)

    for t in range(NT):
        load_x(t).wait()
        rows = pl.ds(t * T, T)
        a[rows] = normed(g[rows])
        keep_a0(t).start()
        acc[rows] = jnp.zeros((T, D), f32)

    forward_x(0, 0)
    forward_x(0, 1)
    forward_y(0, 0)
    both(forward_x, 1)
    forward_y(0, 1)
    arrived(0, 0)
    load_gu(0, 0)
    arrived(0, 1)
    load_d(0, 0)

    def forward_chunk(c, _):
        slot = c % 2
        loaded(slot, 0)
        loaded(slot, 1)

        def body(t, _):
            rows = tile(t)
            gate, up = dot(a[rows], wgu[slot, 0]), dot(a[rows], wgu[slot, 1])
            mid = (gate / (1.0 + jnp.exp(-gate)) * up).astype(bf16)
            acc[rows] += dot(mid, wd[slot])

            @pl.when(t == 1)
            def _():
                both(forward_y, c + 1)
                both(forward_x, c + 2)

            @pl.when(t == 2)
            def _():
                for which in (0, 1):
                    arrived(c + 1, which)
                load_gu(c + 1, 1 - slot)
                load_d(c + 1, 1 - slot)

            return 0

        return lax.fori_loop(0, NT, body, 0)

    lax.fori_loop(0, J, forward_chunk, 0)

    def put_h1(t):
        return pltpu.make_async_copy(g.at[tile(t)], h1_h.at[tile(t)], out_sem.at[t])

    def load_dy(t):
        return pltpu.make_async_copy(dy_h.at[tile(t)], g.at[tile(t)], t_sem.at[t])

    for t in range(NT):
        rows = pl.ds(t * T, T)
        keep_a0(t).wait()
        h1 = (g[rows].astype(f32) + acc[rows].astype(bf16).astype(f32)).astype(bf16)
        g[rows] = h1
        put_h1(t).start()
        a[rows] = normed(h1)
        acc[rows] = jnp.zeros((T, D), f32)
        if t:
            put_h1(t - 1).wait()
            load_dy(t - 1).start()
    put_h1(NT - 1).wait()
    load_dy(NT - 1).start()

    def load_h1(t):
        return pltpu.make_async_copy(h1_h.at[tile(t)], a.at[tile(t)], out_sem.at[t])

    def load_a0(t):
        return pltpu.make_async_copy(a0_h.at[tile(t)], a.at[tile(t)], t_sem.at[t])

    def by_core(p, m):
        return remote(stg.at[p, m, 1 - core], rc.at[p, m], cs.at[p, m], cr.at[p, m], sib)

    def by_x(p, m):
        return remote(xs.at[p, m], rx.at[p, m], xss.at[p, m], xrs.at[p, m], xn)

    def by_y(p, m):
        return remote(ys.at[p, m], ry.at[p, m], yss.at[p, m], yrs.at[p, m], yn)

    def by_z(p, m, k):
        src = zs.at[p, m, of((z + k) % 4 * 80, 80, 80)]
        return remote(src, rz.at[p, m, 3 - k], zss.at[p, m, k - 1], zrs.at[p, m, 3 - k], zn[k])

    def from_z(p, m, k):
        return remote(zs.at[p, m, pl.ds(0, 80)], rz.at[p, m, k - 1], zss.at[p, m, k - 1], zrs.at[p, m, k - 1], zn[k])

    def back_z(c, p, m, k):
        ref = fin.at[c, m, of(320 * y + 80 * z, 80, 80)]
        return remote(ref, ref, ass_.at[p, m, k - 1], ars.at[p, m, 3 - k], zn[k])

    def taken_z(c, p, m, k):
        ref = fin.at[c, m, of(320 * y + 80 * ((z + k) % 4), 80, 80)]
        return remote(ref, ref, ass_.at[p, m, k - 1], ars.at[p, m, k - 1], zn[k])

    def back_y(c, p, m):
        ref = fin.at[c, m, of(320 * y, 320, 320)]
        return remote(ref, ref, bss.at[p, m], brs.at[p, m], yn)

    def s0(c, m, res):
        p = c % 2
        for o in range(4):
            if m == 0:
                stg[p, m, o % 2, o // 2] = res[:, o * COLS : (o + 1) * COLS].astype(bf16)
            else:
                for q in range(4):
                    stg[p, m, o % 2, o // 2, q * ROWS : (q + 1) * ROWS] = res[o * ROWS : (o + 1) * ROWS, q * COLS : (q + 1) * COLS].astype(bf16)
        by_core(p, m).start()

    def s1(c, m):
        p = c % 2
        by_core(p, m).wait()
        xs[p, m] = (stg[p, m, core, 1 - xx].astype(f32) + rc[p, m, 1 - xx].astype(f32)).astype(bf16)
        by_x(p, m).start()

    def s2(c, m):
        p = c % 2
        by_x(p, m).wait()

        def half(h):
            rows = of(320 * h, 320, 320)
            return stg[p, m, core, xx, rows].astype(f32) + rc[p, m, xx, rows].astype(f32) + rx[p, m, rows].astype(f32)

        ys[p, m] = half(1 - y).astype(bf16)
        by_y(p, m).start()
        accy[p, m] = half(y)

    def s3(c, m):
        p = c % 2
        by_y(p, m).wait()
        total = accy[p, m] + ry[p, m].astype(f32)
        accy[p, m] = total
        zs[p, m] = total.astype(bf16)
        for k in (1, 2, 3):
            by_z(p, m, k).start()

    def s4(c, m):
        p = c % 2
        total = accy[p, m, of(80 * z, 80, 80)]
        for k in (1, 2, 3):
            by_z(p, m, k).wait_send()
            from_z(p, m, k).wait_recv()
            total += rz[p, m, k - 1].astype(f32)
        fin[c, m, of(320 * y + 80 * z, 80, 80)] = total.astype(bf16)
        for k in (1, 2, 3):
            back_z(c, p, m, k).start()

    def s5(c, m):
        p = c % 2
        for k in (1, 2, 3):
            back_z(c, p, m, k).wait_send()
            taken_z(c, p, m, k).wait_recv()
        back_y(c, p, m).start()

    def put(c, m):
        return pltpu.make_async_copy(fin.at[c, m], grad_h.at[c, m], o_sem.at[m])

    def s6(c, m):
        p = c % 2
        back_y(c, p, m).wait_send()
        other = fin.at[c, m, of(320 * (1 - y), 320, 320)]
        remote(other, other, bss.at[p, m], brs.at[p, m], yn).wait_recv()
        put(c, m).start()

    def s7(c, m):
        put(c, m).wait()

    SLOTS = {
        "A0": ((s1, 2, 1), (s4, 2, 2), (s5, 0, 2)),
        "A1": ((s2, 0, 1), (s5, 1, 2)),
        "A2": ((s2, 1, 1), (s5, 2, 2), (s6, 0, 2)),
        "A3": ((s2, 2, 1), (s3, 0, 1), (s6, 1, 2)),
        "B0": ((s3, 1, 1), (s6, 2, 2), (s7, 0, 2)),
        "B1": ((s1, 0, 0), (s3, 2, 1), (s4, 0, 1), (s7, 1, 2)),
        "B2": ((s1, 1, 0), (s4, 1, 1), (s7, 2, 2)),
    }
    C = 2 * J

    def run(name, c):
        if isinstance(c, int):
            for fn, m, ago in SLOTS[name]:
                if 0 <= c - ago < C:
                    fn(c - ago, m)
            return
        for back in (0, 1, 2):
            todo = [(fn, m) for fn, m, ago in SLOTS[name] if ago == back]
            if todo and back == 0:
                for fn, m in todo:
                    fn(c, m)
            elif todo:

                @pl.when(c >= back)
                def _(todo=todo, back=back):
                    for fn, m in todo:
                        fn(c - back, m)

    def backward_chunk(c, _):
        slot = c % 2

        @pl.when(c == J)
        def _():
            def body(t, _):
                load_h1(t).wait()
                for i in range(2):
                    rows = of(t * T + i * (T // 2), T // 2, T // 2)
                    wide, by_a = a[rows].astype(f32), acc[rows].astype(bf16).astype(f32)
                    scale = lax.rsqrt(jnp.mean(wide * wide, -1, keepdims=True) + 1e-6)
                    along = jnp.mean(by_a * wide, -1, keepdims=True) * (scale * scale * scale)
                    by_h = (by_a * scale - wide * along).astype(bf16)
                    g[rows] = (g[rows].astype(f32) + by_h.astype(f32)).astype(bf16)
                load_a0(t).start()
                return 0

            lax.fori_loop(0, NT, body, 0)

        loaded(slot, 0)
        loaded(slot, 1)

        def body(t, _):
            rows = tile(t)

            @pl.when(c == 0)
            def _():
                load_dy(t).wait()

            @pl.when(c == J)
            def _():
                load_a0(t).wait()

            gate, up = dot(a[rows], wgu[slot, 0]), dot(a[rows], wgu[slot, 1])
            by_mid = dot(g[rows], wd[slot], TT).astype(bf16).astype(f32)
            sig = 1.0 / (1.0 + jnp.exp(-gate))
            silu = gate * sig
            act[0, rows] = (silu * up).astype(bf16)
            act[2, rows] = (by_mid * silu).astype(bf16)
            act[1, rows] = (by_mid * up * (sig + silu * (1.0 - sig))).astype(bf16)
            for k in range(NT):

                @pl.when(t == k)
                def _(k=k):
                    run(f"A{k}", c)
                    if k < 3:

                        @pl.when(c == 0)
                        def _():
                            both(forward_y, J + 1 + k)
                            if k < 2:
                                both(forward_x, J + 2 + k)
                    else:

                        @pl.when(c + 1 < J)
                        def _():
                            for which in (0, 1):
                                arrived(J + 1 + c, which)

                        @pl.when(c + 1 < C)
                        def _():
                            u = (c + 1 + J) % C
                            load_gu(u, 1 - slot)
                            load_d(u, 1 - slot)

            return 0

        lax.fori_loop(0, NT, body, 0)

        for m, lhs in enumerate((g, a, a)):
            s0(c, m, dot(lhs[...], act[m], TN))
            run(f"B{m}", c)

        @pl.when(c == J - 1)
        def _():
            for t in range(NT):
                load_h1(t).start()

        @pl.when(c < J)
        def _():
            def more(t, _):
                rows = of(t * 2048, 2048, 2048)
                acc[rows] += dot(act[1, rows], wgu[slot, 0], TT) + dot(act[2, rows], wgu[slot, 1], TT)
                return 0

            lax.fori_loop(0, N // 2048, more, 0)

        return 0

    lax.fori_loop(0, C, backward_chunk, 0)

    for c in (C, C + 1):
        for name in SLOTS:
            run(name, c)
    for u in range(2 * J):
        for path in range(5):
            for which in (0, 1):
                gather_copy(u, path, which).wait_send()


def gradients(x, dy, w_gate, w_up, w_down):
    C = L * J
    vmem, dma = pltpu.VMEM, pltpu.SemaphoreType.DMA
    hbm = pl.BlockSpec(memory_space=pl.ANY)
    out = [((C, 2, D, F), bf16), ((C, F, D), bf16), ((N, D), bf16), ((N, D), bf16), ((C, 3, D, COLS), bf16)]
    pair = [dma((2, 3)), dma((2, 3))]
    triple = [dma((2, 3, 3)), dma((2, 3, 3))]
    return pl.pallas_call(
        step_kernel,
        out_shape=[jax.ShapeDtypeStruct(*o) for o in out],
        in_specs=[hbm] * 5,
        out_specs=[hbm] * 5,
        scratch_shapes=[
            vmem((N, D), bf16), vmem((N, D), bf16), vmem((3, N, F), bf16), vmem((N, D), f32),
            vmem((2, 2, D, F), bf16), vmem((2, F, D), bf16),
            vmem((2, 3, 2, 2, D, COLS), bf16), vmem((2, 3, 2, D, COLS), bf16),
            vmem((2, 3, D, COLS), bf16), vmem((2, 3, D, COLS), bf16),
            vmem((2, 3, D // 2, COLS), bf16), vmem((2, 3, D // 2, COLS), bf16), vmem((2, 3, D // 2, COLS), f32),
            vmem((2, 3, D // 2, COLS), bf16), vmem((2, 3, 3, D // 8, COLS), bf16),
            vmem((C, 3, D, COLS), bf16),
            dma((C, 5, 2)), dma((C, 5, 2)), dma((2, 2)), dma((NT,)), dma((NT,)), dma((NT,)),
            *pair, *pair, *pair, *triple, *triple, *pair,
        ],
        compiler_params=pltpu.CompilerParams(collective_id=0, has_side_effects=True, vmem_limit_bytes=67043328),
        cost_estimate=pl.CostEstimate(flops=180 * 10**9, bytes_accessed=10**8, transcendentals=4 * 10**7),
        name="step",
    )(x, dy, w_gate, w_up, w_down)[4]


def adamw_kernel(gg, gu, gd, *refs):
    ins, outs = refs[:9], refs[9:]

    def update(which, at, g):
        w, m, v = (ins[k * 3 + which] for k in range(3))
        g = g.astype(f32)
        new_m = 0.9 * m[at] + 0.1 * g
        new_v = 0.95 * v[at] + 0.05 * g * g
        old = w[at].astype(f32)
        step = new_m * lax.rsqrt(new_v + 1e-8) + 0.1 * old
        outs[which][at] = (old - 0.02 * step).astype(bf16)
        outs[3 + which][at] = new_m
        outs[6 + which][at] = new_v

    for which, grad in enumerate((gg, gu)):
        for j in range(J):
            for q in range(4):
                update(which, (0, slice(None), slice(q * F + j * COLS, q * F + (j + 1) * COLS)), grad[0, j, 0, q])
    for j in range(gd.shape[1]):
        update(2, (0, slice(j * COLS, (j + 1) * COLS), slice(None)), gd[0, j, 0].astype(f32).T)


def adamw(grad, weights, m, v):
    parts = 2
    rows = ROWS // parts
    split = grad.reshape(L, J, 3, 4, ROWS, COLS)
    whole = grad.reshape(L, J, 3, D, COLS)
    ff = pl.BlockSpec((1, rows, FF), lambda l, i: (l, i, 0))
    down = pl.BlockSpec((1, FF // 4 // parts, D), lambda l, i: (l, i, 0))
    three = [ff, ff, down]
    shapes = [jax.ShapeDtypeStruct(o.shape, o.dtype) for o in (*weights, *m, *v)]
    return pl.pallas_call(
        adamw_kernel,
        grid=(L, parts),
        out_shape=shapes,
        in_specs=[
            pl.BlockSpec((1, J, 1, 4, rows, COLS), lambda l, i: (1 - l, 0, 1, 0, i, 0)),
            pl.BlockSpec((1, J, 1, 4, rows, COLS), lambda l, i: (1 - l, 0, 2, 0, i, 0)),
            pl.BlockSpec((1, J // parts, 1, D, COLS), lambda l, i: (1 - l, i, 0, 0, 0)),
            *three, *three, *three,
        ],
        out_specs=[*three, *three, *three],
        compiler_params=pltpu.CompilerParams(vmem_limit_bytes=60 * 2**20),
        name="adamw",
    )(split, split, whole, *weights, *m, *v)


def solution(mesh):
    def step(x, dy, *arrays):
        weights, m, v = (arrays[i : i + 3] for i in (0, 3, 6))
        grad = gradients(x[0], dy[0], *weights)
        return tuple(adamw(grad, weights, m, v))

    states, cut = P(("rep", "r", "s"), None, None), P(None, "s", None)
    return jax.shard_map(
        step,
        mesh=mesh,
        in_specs=(states, states) + (cut,) * 9,
        out_specs=(P("rep", "s", None),) * 9,
        check_vma=False,
    )
```

time: 698 us -> 326 us (0.47)
  matrix products: 366 us -> 0 us
  Pallas kernels: 0 us -> 325 us
  waiting for transfers between devices: 256 us -> 0 us
  other arithmetic: 29.7 us -> 0 us
  local copies, waits for them, and re-layouts: 24.6 us -> 0 us
  between operations: 14.5 us -> 0.83 us
    dot_general x15 -> x0, matrix products: 366 us -> none  [the longest x5 136 us: layer(): gate = jnp.dot(a, w['w_gate'], preferred_element_type=jnp.float32)]
    pallas_call x0 -> x2, Pallas kernels: none -> 325 us  [the longest x1 310 us: gradients(): pl.pallas_call(step_kernel, out_shape=[jax.ShapeDtypeStruct(*o) for o in...]
    psum x1 -> x0, waiting for transfers between devices: 153 us -> none  [summed(): lax.psum(lax.psum_scatter(term, 's', scatter_dimension=0, tiled=True), 'r')]
    reduce_scatter x6 -> x0, waiting for transfers between devices: 77.5 us -> none  [summed(): lax.psum_scatter(term, 's', scatter_dimension=0, tiled=True)]
    all_gather x6 -> x0, waiting for transfers between devices: 23.5 us -> none  [fetched(): lax.all_gather(w[number], 's', axis=0, tiled=True)]
    unnamed x38 -> x0, local copies, waits for them, and re-layouts: 18.3 us -> none
    convert_element_type x2 -> x0, other arithmetic: 14.2 us -> none  [adamw(): return ((w - 0.02 * step).astype(jnp.bfloat16), m, v)]
    add_any x1 -> x0, other arithmetic: 11.9 us -> none  [normed(): wide = h.astype(jnp.float32)]
  transfers between devices with their start and end apart: 13 -> 0, of which waited for: 9 -> 0; matrix products, arithmetic and copies ran while one was open for 41% -> 0% of each run, Pallas kernels for 0% -> 0%
where the time goes in v1:
time: 326 us
  Pallas kernels  325 us (100%)
    pallas_call x1, Pallas kernels, gradients(): pl.pallas_call(step_kernel, out_shape=[jax.ShapeDtypeStruct(*o) for o in...  310 us
    pallas_call x1, Pallas kernels, adamw(): pl.pallas_call(adamw_kernel, grid=(L, parts), out_shape=shapes, in_specs=...  14.8 us

profile of v1, /device:TPU:0, one launch (start us, length us, event | category | flops | bytes accessed | tf_op | source)
XLA Modules:
  0.0 325.6 jit_solution(9037257401415670198)
XLA Ops:
  0.6 310.0 %step.1 = (bf16[8,2,640,512]{3,2,1,0:T(8,128)(2,1)}, bf16[8,512,640]{2,1,0:T(8,128)(2,1)}, bf16[4096,640]{1,0:T(8,128)(2,1)}, bf16[4096,640]{1,0:T(8,128)(2,1)}, bf16[8,3,640,128]{3,2,1,0:T(8,128)(2,1)}) custom-call(bf16[4096,640]{1,0:T(8,128)(2,1)} %bitcast.7, bf16[4096,640]{1,0:T(8,128)(2,1)} %bitcast.8, bf16[2,160,2048]{2,1,0:T(8,128)(2,1)} %refs_0_.1, ...), custom_call_target="tpu_custom_call" | custom-call | flops 179999997952 | bytes 100000000 | tf_op jit(solution)/shard_map/step/pallas_call | solution.py:442
  310.6 14.8 %adamw.1 = (bf16[2,160,2048]{2,1,0:T(8,128)(2,1)}, bf16[2,160,2048]{2,1,0:T(8,128)(2,1)}, bf16[2,512,640]{2,1,0:T(8,128)(2,1)}, f32[2,160,2048]{2,1,0:T(8,128)},...) custom-call(bf16[2,4,3,4,160,128]{5,4,3,2,1,0:T(8,128)(2,1)} %bitcas, ...), custom_call_target="tpu_custom_call" | custom-call | tf_op jit(solution)/shard_map/adamw/pallas_call | solution.py:495

commit v2 on v1

v2 whole, which is shorter than its diff:
```python
import functools

import jax
import jax.numpy as jnp
from jax import lax
from jax.experimental import pallas as pl
from jax.experimental.pallas import tpu as pltpu
from jax.sharding import PartitionSpec as P

MESH = pl.DeviceIdType.MESH
f32, bf16 = jnp.float32, jnp.bfloat16
N, D, FF, L = 4096, 640, 2048, 2
F = 512
J = FF // F
T = 1024
NT = N // T
SUB = 256
HALVES = (pl.ds(0, SUB), pl.ds(SUB, SUB))
HALF, BLOCK = D // 2, D // 8
VLIM = 62
ROWS, COLS = D // 4, F // 4
NN, TN, TT = (((1,), (0,)), ((), ())), (((0,), (0,)), ((), ())), (((1,), (1,)), ((), ()))


def dot(a, b, dims=NN):
    return lax.dot_general(a, b, dims, preferred_element_type=f32)


def of(start, size):
    return pl.ds(pl.multiple_of(start, size), size)


def normed(h):
    wide = h.astype(f32)
    return (wide * lax.rsqrt(jnp.mean(wide * wide, -1, keepdims=True) + 1e-6)).astype(bf16)


def step_kernel(
    x_h, dy_h, wg_h, wu_h, wd_h,
    ggu_h, gd_h, h1_h, a0_h, gates_h, mids_h, grad_h,
    a, g, acc, half, wgu, wd, stg, rc, xs, rx, ys, ry, accy, zs, rz, fin,
    gs_sem, gr_sem, gs0, gr0, own0, save_sem, w_sem, t_sem, o_sem, out_sem, gate_sem, mid_sem,
    put_sem, cs, cr, xss, xrs, yss, yrs, zss, zrs, ass_, ars, bss, brs,
):
    C = 2 * J
    s, r = lax.axis_index("s"), lax.axis_index("r")
    xx, core = s // 2, s % 2
    y, z = r // 4, r % 4
    sib, xn = {"s": 2 * xx + 1 - core}, {"s": 2 * (1 - xx) + core}
    yn = {"r": 4 * (1 - y) + z}
    zn = {k: {"r": 4 * y + (z + k) % 4} for k in (1, 2, 3)}

    def remote(src, dst, ss, rs, to):
        return pltpu.make_async_remote_copy(src_ref=src, dst_ref=dst, send_sem=ss, recv_sem=rs, device_id=to, device_id_type=MESH)

    barrier = pltpu.get_barrier_semaphore()
    for peer in (sib, xn, yn, zn[1], zn[2], zn[3]):
        pl.semaphore_signal(barrier, inc=1, device_id=peer, device_id_type=MESH)

    def tile(t):
        return of(t * T, T)

    def load_x(t):
        return pltpu.make_async_copy(x_h.at[tile(t)], g.at[tile(t)], t_sem.at[t])

    def keep_a0(t):
        return pltpu.make_async_copy(a.at[tile(t)], a0_h.at[tile(t)], o_sem.at[t])

    def part_0(which, owner, h=None):
        if which < 2:
            return wgu.at[0, which, of(owner * ROWS, ROWS), pl.ds(0, F) if h is None else of(SUB * h, SUB)]
        return wd.at[0, of(owner * COLS, COLS) if h is None else of(owner * COLS + COLS // 2 * h, COLS // 2)]

    for which, w in enumerate((wg_h, wu_h)):
        for b in range(4):
            cols = pl.ds(b * COLS, COLS)
            pltpu.make_async_copy(w.at[0, :, pl.ds(b * F, COLS)], wgu.at[0, which, of(s * ROWS, ROWS), cols], own0.at[which]).start()
    pltpu.make_async_copy(wd_h.at[0, pl.ds(0, COLS)], part_0(2, s), own0.at[2]).start()

    def route(path):
        theirs = xn["s"]
        return ((s, None, sib), (s, y, xn), (theirs, y, yn), (theirs, y, sib), (theirs, 1 - y, sib))[path]

    def copy_0(path, which):
        owner, h, to = route(path)
        ref = part_0(which, owner, h)
        return remote(ref, ref, gs0.at[path, which], gr0.at[path, which], to)

    for t in range(NT):
        load_x(t).start()
    pl.semaphore_wait(barrier, 6)
    for which in range(3):
        pltpu.make_async_copy(part_0(which, s), part_0(which, s), own0.at[which]).wait()
        copy_0(1, which).start()
        copy_0(0, which).start()

    def part_gu(u, owner, h=None):
        cols = pl.ds(0, F) if h is None else of(SUB * h, SUB)
        return ggu_h.at[u, :, of(owner * ROWS, ROWS), cols]

    def part_d(u, owner, h=None):
        rows = of(owner * COLS, COLS) if h is None else of(owner * COLS + COLS // 2 * h, COLS // 2)
        return gd_h.at[u, rows]

    def own_pieces(u, blocks):
        layer, j = u // J, u % J
        for which, w in enumerate((wg_h, wu_h)):
            for b in blocks:
                yield w.at[layer, :, of(b * F + j * COLS, COLS)], which, of(b * COLS, COLS)

    def own_d(u, h=None):
        layer, j = u // J, u % J
        rows = of(j * COLS, COLS) if h is None else of(j * COLS + COLS // 2 * h, COLS // 2)
        return wd_h.at[layer, rows]

    def send_own(u):
        for h, path, to in ((y, 1, xn), (None, 0, sib)):
            blocks = range(4) if h is None else (2 * h, 2 * h + 1)
            for src, which, cols in own_pieces(u, blocks):
                remote(src, ggu_h.at[u, which, of(s * ROWS, ROWS), cols], gs_sem.at[path, 0], gr_sem.at[u, path, 0], to).start()
            remote(own_d(u, h), part_d(u, s, h), gs_sem.at[path, 1], gr_sem.at[u, path, 1], to).start()

    def gather_copy(u, path, which):
        owner, h, to = route(path)
        ref = (part_gu, part_d)[which](u, owner, h)
        return remote(ref, ref, gs_sem.at[path, which], gr_sem.at[u, path, which], to)

    def gather_sent(path, which):
        owner, h, to = route(path)
        ref = (part_gu, part_d)[which](pl.ds(1, C - 1), owner, h)
        remote(ref, ref, gs_sem.at[path, which], gr_sem.at[0, path, which], to).wait_send()

    def forward_x(u, which):
        gather_copy(u, 1, which).wait_recv()
        gather_copy(u, 2, which).start()
        gather_copy(u, 3, which).start()

    def forward_y(u, which):
        gather_copy(u, 2, which).wait_recv()
        gather_copy(u, 4, which).start()

    def both(fn, u):
        fn(u, 0)
        fn(u, 1)

    def arrived(u, which):
        for path in (0, 3, 4):
            gather_copy(u, path, which).wait_recv()

    def load_gu(u, slot):
        for src, which, cols in own_pieces(u, range(4)):
            pltpu.make_async_copy(src, wgu.at[slot, which, of(s * ROWS, ROWS), cols], w_sem.at[slot, 0]).start()
        for k in (1, 2, 3):
            owner = (s + k) % 4
            pltpu.make_async_copy(part_gu(u, owner), wgu.at[slot, :, of(owner * ROWS, ROWS)], w_sem.at[slot, 0]).start()

    def load_d(u, slot):
        pltpu.make_async_copy(own_d(u), wd.at[slot, of(s * COLS, COLS)], w_sem.at[slot, 1]).start()
        for k in (1, 2, 3):
            owner = (s + k) % 4
            pltpu.make_async_copy(part_d(u, owner), wd.at[slot, of(owner * COLS, COLS)], w_sem.at[slot, 1]).start()

    def loaded(slot, which):
        ref = (wgu, wd)[which].at[slot]
        pltpu.make_async_copy(ref, ref, w_sem.at[slot, which]).wait()

    for u in range(1, 2 * J):
        send_own(u)

    for t in range(NT):
        load_x(t).wait()
        rows = pl.ds(t * T, T)
        a[rows] = normed(g[rows])
        keep_a0(t).start()
        acc[rows] = jnp.zeros((T, D), f32)

    def forward_x0(which):
        copy_0(1, which).wait_recv()
        copy_0(2, which).start()
        copy_0(3, which).start()

    def forward_y0(which):
        copy_0(2, which).wait_recv()
        copy_0(4, which).start()

    with jax.named_scope("w0"):
        for which in range(3):
            forward_x0(which)
        for which in range(2):
            forward_y0(which)
        for which in range(2):
            for path in (0, 3, 4):
                copy_0(path, which).wait_recv()
    save_0 = (
        pltpu.make_async_copy(wgu.at[0], ggu_h.at[0], save_sem.at[0]),
        pltpu.make_async_copy(wd.at[0], gd_h.at[0], save_sem.at[1]),
    )
    save_0[0].start()

    def forward(kept, mid):
        def keep(c, t):
            return pltpu.make_async_copy(kept.at[t % 2], gates_h.at[c, :, tile(t)], gate_sem.at[t % 2])

        def keep_mid(c, t):
            return pltpu.make_async_copy(mid.at[tile(t)], mids_h.at[c, tile(t)], mid_sem.at[t])

        def chunk(c, _):
            slot = c % 2

            @pl.when(c > 0)
            def _():
                with jax.named_scope("wload"):
                    loaded(slot, 0)

            def body(t, _):
                @pl.when(c * NT + t >= 2)
                def _():
                    keep(c, t).wait()

                @pl.when(c > 0)
                def _():
                    keep_mid(c, t).wait()

                with jax.named_scope("ftile"):
                    for i in range(T // SUB):
                        rows, part = of(t * T + i * SUB, SUB), pl.ds(i * SUB, SUB)
                        for cols in HALVES:
                            gate, up = dot(a[rows], wgu[slot, 0, :, cols]), dot(a[rows], wgu[slot, 1, :, cols])
                            sig = 1.0 / (1.0 + jnp.exp(-gate))
                            silu = gate * sig
                            kept[t % 2, 0, part, cols] = silu
                            kept[t % 2, 1, part, cols] = up * (sig + silu * (1.0 - sig))
                            mid[rows, cols] = (silu * up).astype(bf16)
                keep_mid(c, t).start()
                keep(c, t).start()

                @pl.when((t == 0) & (c == 0))
                def _():
                    with jax.named_scope("f0"):
                        forward_y0(2)
                        forward_x(1, 0)

                @pl.when((t == 1) & (c == 0))
                def _():
                    with jax.named_scope("f1"):
                        forward_x(1, 1)

                @pl.when((t == 1) & (c > 0))
                def _():
                    with jax.named_scope("fa"):
                        arrived(c, 1)
                        load_d(c, slot)

                @pl.when(t == NT - 1)
                def _():
                    with jax.named_scope("f3"):
                        forward_y(c + 1, 0)

                return 0

            lax.fori_loop(0, NT, body, 0)

            def middle():
                with jax.named_scope("mid"):
                    forward_y(c + 1, 1)
                    arrived(c + 1, 0)

                    @pl.when(c == 1)
                    def _():
                        for copy in save_0:
                            copy.wait()
                        for path in range(5):
                            for which in range(3):
                                copy_0(path, which).wait_send()

                    load_gu(c + 1, 1 - slot)
                    both(forward_x, c + 2)

            @pl.when(c == 0)
            def _():
                for path in (0, 3, 4):
                    copy_0(path, 2).wait_recv()
                save_0[1].start()

            @pl.when(c > 0)
            def _():
                with jax.named_scope("wload"):
                    loaded(slot, 1)

            @pl.when(c < J - 1)
            def _():
                def down(t, _):
                    rows = of(t * 2 * T, 2 * T)
                    acc[rows] += dot(mid[rows], wd[slot])
                    pl.when(t == 0)(middle)
                    return 0

                with jax.named_scope("fdown"):
                    lax.fori_loop(0, N // (2 * T), down, 0)

            @pl.when(c == J - 1)
            def _():
                def down(t, _):
                    keep_a0(t).wait()
                    for i in range(4):
                        rows = of(t * T + i * SUB, SUB)
                        add = (acc[rows] + dot(mid[rows], wd[slot])).astype(bf16)
                        h1 = (g[rows].astype(f32) + add.astype(f32)).astype(bf16)
                        g[rows] = h1
                        a[rows] = normed(h1)
                        acc[rows] = jnp.zeros((SUB, D), f32)
                    put_h1(t).start()
                    pl.when(t == 1)(middle)

                    @pl.when(t > 0)
                    def _():
                        put_h1(t - 1).wait()
                        load_dy(t - 1).start()

                    return 0

                with jax.named_scope("fdown1"):
                    lax.fori_loop(0, NT, down, 0)
                arrived(J, 1)
                load_d(J, 0)

            return 0

        lax.fori_loop(0, J, chunk, 0)
        for t in range(NT):
            keep_mid(J - 1, t).wait()
        keep(J - 1, 0).wait()
        keep(J - 1, 1).wait()

    def put_h1(t):
        return pltpu.make_async_copy(g.at[tile(t)], h1_h.at[tile(t)], out_sem.at[t])

    def load_dy(t):
        return pltpu.make_async_copy(dy_h.at[tile(t)], g.at[tile(t)], t_sem.at[t])

    def load_h1(t):
        return pltpu.make_async_copy(h1_h.at[tile(t)], a.at[tile(t)], out_sem.at[t])

    def load_a0(t):
        return pltpu.make_async_copy(a0_h.at[tile(t)], a.at[tile(t)], t_sem.at[t])

    pl.run_scoped(forward, pltpu.VMEM((2, 2, T, F), f32), pltpu.VMEM((N, F), bf16))
    put_h1(NT - 1).wait()
    load_dy(NT - 1).start()

    def by_core(p, m):
        return remote(stg.at[p, m, 1 - core], rc.at[p, m], cs.at[p, m], cr.at[p, m], sib)

    def by_x(p, m):
        return remote(xs.at[p, m], rx.at[p, m], xss.at[p, m], xrs.at[p, m], xn)

    def by_y(p, m):
        return remote(ys.at[p, m], ry.at[p, m], yss.at[p, m], yrs.at[p, m], yn)

    def by_z(p, m, k):
        return remote(zs.at[p, m, of((z + k) % 4 * BLOCK, BLOCK)], rz.at[p, m, 3 - k], zss.at[p, m], zrs.at[p, m], zn[k])

    def by_z_all(p, m):
        return remote(zs.at[p, m, pl.ds(0, 3 * BLOCK)], rz.at[p, m], zss.at[p, m], zrs.at[p, m], zn[1])

    def back_z(c, p, m, k):
        ref = fin.at[c, m, of(HALF * y + BLOCK * z, BLOCK)]
        return remote(ref, ref, ass_.at[p, m], ars.at[p, m], zn[k])

    def back_z_all(c, p, m):
        ref = fin.at[c, m, pl.ds(0, 3 * BLOCK)]
        return remote(ref, ref, ass_.at[p, m], ars.at[p, m], zn[1])

    def back_y(c, p, m):
        ref = fin.at[c, m, of(HALF * y, HALF)]
        return remote(ref, ref, bss.at[p, m], brs.at[p, m], yn)

    def s0(c, m, res):
        p = c % 2
        for o in range(4):
            if m == 0:
                stg[p, m, o % 2, o // 2] = res[:, o * COLS : (o + 1) * COLS].astype(bf16)
            else:
                for q in range(4):
                    stg[p, m, o % 2, o // 2, q * ROWS : (q + 1) * ROWS] = res[o * ROWS : (o + 1) * ROWS, q * COLS : (q + 1) * COLS].astype(bf16)
        by_core(p, m).start()

    def s1(c, m):
        p = c % 2
        by_core(p, m).wait()
        xs[p, m] = (stg[p, m, core, 1 - xx].astype(f32) + rc[p, m, 1 - xx].astype(f32)).astype(bf16)
        by_x(p, m).start()

    def s2(c, m):
        p = c % 2
        by_x(p, m).wait()

        def sum_of(h):
            rows = of(HALF * h, HALF)
            return stg[p, m, core, xx, rows].astype(f32) + rc[p, m, xx, rows].astype(f32) + rx[p, m, rows].astype(f32)

        ys[p, m] = sum_of(1 - y).astype(bf16)
        by_y(p, m).start()
        accy[p, m] = sum_of(y)

    def s3(c, m):
        p = c % 2
        by_y(p, m).wait()
        total = accy[p, m] + ry[p, m].astype(f32)
        accy[p, m] = total
        zs[p, m] = total.astype(bf16)
        for k in zn:
            by_z(p, m, k).start()

    def s4(c, m):
        p = c % 2
        by_z_all(p, m).wait_send()
        by_z_all(p, m).wait_recv()
        total = accy[p, m, of(BLOCK * z, BLOCK)]
        for k in range(3):
            total += rz[p, m, k].astype(f32)
        fin[c, m, of(HALF * y + BLOCK * z, BLOCK)] = total.astype(bf16)
        for k in zn:
            back_z(c, p, m, k).start()

    def s5(c, m):
        p = c % 2
        back_z_all(c, p, m).wait()
        back_y(c, p, m).start()

    def put(c, m):
        return pltpu.make_async_copy(fin.at[c, m], grad_h.at[c, m], put_sem.at[0])

    def s6(c, m):
        p = c % 2
        back_y(c, p, m).wait_send()
        other = fin.at[c, m, of(HALF * (1 - y), HALF)]
        remote(other, other, bss.at[p, m], brs.at[p, m], yn).wait_recv()
        put(c, m).start()

    SLOTS = {
        "A0": "201",
        "A1": "121 412 623",
        "A2": "211",
        "A3": "",
        "H0": "502",
        "H1": "301 422",
        "H2": "100 221 512 602",
        "H3": "311",
        "H4": "110 401 522",
        "H5": "321 612",
    }
    STEPS = (None, s1, s2, s3, s4, s5, s6)
    SLOTS = {name: [tuple(map(int, word)) for word in words.split()] for name, words in SLOTS.items()}

    def run(name, c):
        with jax.named_scope("slot_" + name):
            for back in range(4):
                todo = [(STEPS[i], m) for i, m, ago in SLOTS[name] if ago == back]

                def do(todo=todo, back=back):
                    for fn, m in todo:
                        fn(c - back, m)

                if todo and back:
                    pl.when(c >= back)(do)
                elif todo:
                    do()

    def ready(i, m, c):
        start, by_x_done = ((-4.3, 1.4), (-1.4, 4.9), (1.8, 8.4))[m]
        after = start if i == 1 else by_x_done + (0.0, 4.0, 9.3, 14.6, 18.6)[i - 2]
        return after if c == C - 1 else after + 6.0 - 13.0 * (C - 1 - c)

    def finish():
        left = sorted((ready(i, m, c), i, m, c) for events in SLOTS.values() for i, m, ago in events for c in range(C - ago, C))
        sent = [(path, which) for path in range(5) for which in range(2)]
        for n, (_, i, m, c) in enumerate(left):
            with jax.named_scope(f"t{i}_{m}_{c}"):
                STEPS[i](c, m)
            if n < len(sent):
                gather_sent(*sent[n])
        pltpu.make_async_copy(fin, grad_h, put_sem.at[0]).wait()

    def gates(t):
        half = (t % 2) * 2 * T
        return acc.at[of(half, T), pl.ds(0, F)], acc.at[of(half + T, T), pl.ds(0, F)]

    def load_gates(c, t):
        return [
            pltpu.make_async_copy(gates_h.at[c - J, which, tile(t)], to, gate_sem.at[which * 2 + t % 2])
            for which, to in enumerate(gates(t))
        ]

    def backward(act):
        def chunk(c, _):
            slot = c % 2
            with jax.named_scope("wload"):
                loaded(slot, 0)
                loaded(slot, 1)

            def by_gates(rows, cols, gate, up, by_mid):
                by_mid = by_mid.astype(bf16).astype(f32)
                sig = 1.0 / (1.0 + jnp.exp(-gate))
                silu = gate * sig
                act[0, rows, cols] = (silu * up).astype(bf16)
                act[2, rows, cols] = (by_mid * silu).astype(bf16)
                act[1, rows, cols] = (by_mid * up * (sig + silu * (1.0 - sig))).astype(bf16)

            def load_mids(chunk, t):
                return pltpu.make_async_copy(mids_h.at[chunk - J, tile(t)], act.at[0, tile(t)], mid_sem.at[t])

            def product(m, h):
                lhs, rows = (g, a, a)[m], pl.ds(h * (N // 2), N // 2)
                with jax.named_scope(f"dw{m}{h}"):
                    if h == 0:
                        half[...] = dot(lhs[rows], act[m, rows], TN)
                    else:
                        s0(c, m, half[...] + dot(lhs[rows], act[m, rows], TN))
                run(f"H{2 * m + h}", c)
                if m < h:

                    @pl.when((c >= J - 1) & (c < C - 1))
                    def _():
                        for t in range(NT):
                            load_mids(c + 1, t).start()

            def body(t, _):
                @pl.when(c < J)
                def _():
                    @pl.when(c == 0)
                    def _():
                        load_dy(t).wait()

                    with jax.named_scope("btile"):
                        for i in range(4):
                            rows = of(t * T + i * SUB, SUB)
                            for cols in HALVES:
                                gate, up = dot(a[rows], wgu[slot, 0, :, cols]), dot(a[rows], wgu[slot, 1, :, cols])
                                by_gates(rows, cols, gate, up, dot(g[rows], wd[slot, cols], TT))

                @pl.when(c >= J)
                def _():
                    with jax.named_scope("gwait"):
                        for copy in load_gates(c, t):
                            copy.wait()
                    with jax.named_scope("ctile"):
                        by_up, by_gate = gates(t)
                        for i in range(T // SUB):
                            rows, part = of(t * T + i * SUB, SUB), pl.ds(i * SUB, SUB)
                            by_mid = dot(g[rows], wd[slot], TT).astype(bf16).astype(f32)
                            act[2, rows] = (by_mid * by_up[part]).astype(bf16)
                            act[1, rows] = (by_mid * by_gate[part]).astype(bf16)

                    @pl.when(t < 2)
                    def _():
                        for copy in load_gates(c, t + 2):
                            copy.start()

                    @pl.when((t >= 2) & (c + 1 < C))
                    def _():
                        for copy in load_gates(c + 1, t - 2):
                            copy.start()

                for k in range(NT):

                    @pl.when(t == k)
                    def _(k=k):
                        run(f"A{k}", c)
                        if k in (1, 2):

                            @pl.when(c >= J)
                            def _():
                                if k == 1:
                                    for t in range(NT):
                                        load_mids(c, t).wait()
                                product(0, k - 1)

                        if k < 3:

                            @pl.when(c == 0)
                            def _():
                                if k == 0:
                                    both(forward_y, J + 1)
                                    both(forward_x, J + 2)
                                if k == 2:
                                    both(forward_x, J + 3)

                            if k == 1:

                                @pl.when(c == 1)
                                def _():
                                    both(forward_y, J + 3)

                        else:

                            @pl.when(c == 0)
                            def _():
                                both(forward_y, J + 2)

                            @pl.when(c + 1 < J)
                            def _():
                                for which in (0, 1):
                                    arrived(J + 1 + c, which)

                            @pl.when(c + 1 < C)
                            def _():
                                u = (c + 1 + J) % C
                                load_gu(u, 1 - slot)
                                load_d(u, 1 - slot)

                return 0

            lax.fori_loop(0, NT, body, 0)

            @pl.when(c == J)
            def _():
                for t in range(NT):
                    load_a0(t).wait()

            for m in range(3):
                for h in range(2):
                    if m:
                        product(m, h)
                    else:
                        pl.when(c < J)(functools.partial(product, m, h))

            def by_states(rows):
                return dot(act[1, rows], wgu[slot, 0], TT) + dot(act[2, rows], wgu[slot, 1], TT)

            @pl.when(c < J - 1)
            def _():
                def more(t, _):
                    for i in range(8):
                        rows = of(t * 2 * T + i * SUB, SUB)
                        acc[rows] += by_states(rows)
                    return 0

                with jax.named_scope("p3"):
                    lax.fori_loop(0, N // (2 * T), more, 0)

            @pl.when(c == J - 1)
            def _():
                for t in range(NT):
                    load_h1(t).start()

                def more(t, _):
                    load_h1(t).wait()
                    for i in range(4):
                        rows = of(t * T + i * SUB, SUB)
                        by_a = (acc[rows] + by_states(rows)).astype(bf16).astype(f32)
                        wide = a[rows].astype(f32)
                        scale = lax.rsqrt(jnp.mean(wide * wide, -1, keepdims=True) + 1e-6)
                        along = jnp.mean(by_a * wide, -1, keepdims=True) * (scale * scale * scale)
                        by_h = (by_a * scale - wide * along).astype(bf16)
                        g[rows] = (g[rows].astype(f32) + by_h.astype(f32)).astype(bf16)
                    load_a0(t).start()

                    @pl.when(t % 2 == 1)
                    def _():
                        for copy in load_gates(J, t // 2):
                            copy.start()

                    return 0

                with jax.named_scope("normbwd"):
                    lax.fori_loop(0, NT, more, 0)

            return 0

        lax.fori_loop(0, C, chunk, 0)

    pl.run_scoped(backward, pltpu.VMEM((3, N, F), bf16))
    finish()


def gradients(x, dy, w_gate, w_up, w_down):
    C = L * J
    vmem, dma = pltpu.VMEM, pltpu.SemaphoreType.DMA
    hbm = pl.BlockSpec(memory_space=pl.ANY)
    out = [((C, 2, D, F), bf16), ((C, F, D), bf16), ((N, D), bf16), ((N, D), bf16), ((J, 2, N, F), f32), ((J, N, F), bf16), ((C, 3, D, COLS), bf16)]
    pairs = [dma((2, 3))] * 12
    return pl.pallas_call(
        step_kernel,
        out_shape=[jax.ShapeDtypeStruct(*o) for o in out],
        in_specs=[hbm] * 5,
        out_specs=[hbm] * 7,
        scratch_shapes=[
            vmem((N, D), bf16), vmem((N, D), bf16), vmem((N, D), f32), vmem((D, F), f32),
            vmem((2, 2, D, F), bf16), vmem((2, F, D), bf16),
            vmem((2, 3, 2, 2, D, COLS), bf16), vmem((2, 3, 2, D, COLS), bf16),
            vmem((2, 3, D, COLS), bf16), vmem((2, 3, D, COLS), bf16),
            vmem((2, 3, D // 2, COLS), bf16), vmem((2, 3, D // 2, COLS), bf16), vmem((2, 3, D // 2, COLS), f32),
            vmem((2, 3, D // 2, COLS), bf16), vmem((2, 3, 3, D // 8, COLS), bf16),
            vmem((C, 3, D, COLS), bf16),
            dma((5, 2)), dma((C, 5, 2)), dma((5, 3)), dma((5, 3)), dma((3,)), dma((2,)), dma((2, 2)), dma((NT,)), dma((NT,)), dma((NT,)), dma((4,)), dma((NT,)), dma((1,)),
            *pairs,
        ],
        compiler_params=pltpu.CompilerParams(collective_id=0, has_side_effects=True, vmem_limit_bytes=VLIM * 2**20),
        cost_estimate=pl.CostEstimate(flops=180 * 10**9, bytes_accessed=10**8, transcendentals=4 * 10**7),
        name="step",
    )(x, dy, w_gate, w_up, w_down)[6]


def adamw_kernel(gg, gu, gd, *refs):
    ins, outs = refs[:9], refs[9:]

    def update(which, at, g):
        w, m, v = (ins[k * 3 + which] for k in range(3))
        g = g.astype(f32)
        new_m = 0.9 * m[at] + 0.1 * g
        new_v = 0.95 * v[at] + 0.05 * g * g
        old = w[at].astype(f32)
        step = new_m * lax.rsqrt(new_v + 1e-8) + 0.1 * old
        outs[which][at] = (old - 0.02 * step).astype(bf16)
        outs[3 + which][at] = new_m
        outs[6 + which][at] = new_v

    for which, grad in enumerate((gg, gu)):
        for j in range(J):
            for q in range(4):
                update(which, (0, slice(None), slice(q * F + j * COLS, q * F + (j + 1) * COLS)), grad[0, j, 0, q])
    for j in range(gd.shape[1]):
        update(2, (0, slice(j * COLS, (j + 1) * COLS), slice(None)), gd[0, j, 0].astype(f32).T)


def adamw(grad, weights, m, v):
    parts = 2
    rows = ROWS // parts
    split = grad.reshape(L, J, 3, 4, ROWS, COLS)
    whole = grad.reshape(L, J, 3, D, COLS)
    ff = pl.BlockSpec((1, rows, FF), lambda l, i: (l, i, 0))
    down = pl.BlockSpec((1, FF // 4 // parts, D), lambda l, i: (l, i, 0))
    three = [ff, ff, down]
    shapes = [jax.ShapeDtypeStruct(o.shape, o.dtype) for o in (*weights, *m, *v)]
    return pl.pallas_call(
        adamw_kernel,
        grid=(L, parts),
        out_shape=shapes,
        in_specs=[
            pl.BlockSpec((1, J, 1, 4, rows, COLS), lambda l, i: (1 - l, 0, 1, 0, i, 0)),
            pl.BlockSpec((1, J, 1, 4, rows, COLS), lambda l, i: (1 - l, 0, 2, 0, i, 0)),
            pl.BlockSpec((1, J // parts, 1, D, COLS), lambda l, i: (1 - l, i, 0, 0, 0)),
            *three, *three, *three,
        ],
        out_specs=[*three, *three, *three],
        compiler_params=pltpu.CompilerParams(vmem_limit_bytes=56 * 2**20),
        name="adamw",
    )(split, split, whole, *weights, *m, *v)


def solution(mesh):
    def step(x, dy, *arrays):
        weights, m, v = (arrays[i : i + 3] for i in (0, 3, 6))
        grad = gradients(x[0], dy[0], *weights)
        return tuple(adamw(grad, weights, m, v))

    states, cut = P(("rep", "r", "s"), None, None), P(None, "s", None)
    return jax.shard_map(
        step,
        mesh=mesh,
        in_specs=(states, states) + (cut,) * 9,
        out_specs=(P("rep", "s", None),) * 9,
        check_vma=False,
    )
```

time: 326 us -> 289 us (0.89)
  Pallas kernels: 325 us -> 288 us
    pallas_call x1, Pallas kernels: 310 us -> 273 us  [gradients(): pl.pallas_call(step_kernel, out_shape=[jax.ShapeDtypeStruct(*o) for o in...]
where the time goes in v2:
time: 289 us
  Pallas kernels  288 us (100%)
    pallas_call x1, Pallas kernels, gradients(): pl.pallas_call(step_kernel, out_shape=[jax.ShapeDtypeStruct(*o) for o in...  273 us
    pallas_call x1, Pallas kernels, adamw(): pl.pallas_call(adamw_kernel, grid=(L, parts), out_shape=shapes, in_specs=...  14.8 us

profile of v2, /device:TPU:0, one launch (start us, length us, event | category | flops | bytes accessed | tf_op | source)
XLA Modules:
  0.0 289.0 jit_solution(13304954127683237579)
XLA Ops:
  0.6 273.3 %step.1 = (bf16[8,2,640,512]{3,2,1,0:T(8,128)(2,1)}, bf16[8,512,640]{2,1,0:T(8,128)(2,1)}, bf16[4096,640]{1,0:T(8,128)(2,1)}, bf16[4096,640]{1,0:T(8,128)(2,1)},...) custom-call(bf16[4096,640]{1,0:T(8,128)(2,1)} %bitcast.7, ...), custom_call_target="tpu_custom_call" | custom-call | flops 179999997952 | bytes 100000000 | tf_op jit(solution)/shard_map/step/pallas_call | solution.py:683
  273.9 14.8 %adamw.1 = (bf16[2,160,2048]{2,1,0:T(8,128)(2,1)}, bf16[2,160,2048]{2,1,0:T(8,128)(2,1)}, bf16[2,512,640]{2,1,0:T(8,128)(2,1)}, f32[2,160,2048]{2,1,0:T(8,128)},...) custom-call(bf16[2,4,3,4,160,128]{5,4,3,2,1,0:T(8,128)(2,1)} %bitcas, ...), custom_call_target="tpu_custom_call" | custom-call | tf_op jit(solution)/shard_map/adamw/pallas_call | solution.py:736

commit v3 on v2

--- a/solution.py
+++ b/solution.py
@@ -201,6 +201,11 @@
         def keep(c, t):
             return pltpu.make_async_copy(kept.at[t % 2], gates_h.at[c, :, tile(t)], gate_sem.at[t % 2])
 
+        def keep_half(c, t, h):
+            rows, size = h * (T // 2), T // 2
+            to = gates_h.at[c, :, of(t * T + rows, size)]
+            return pltpu.make_async_copy(kept.at[t % 2, :, pl.ds(rows, size)], to, gate_sem.at[t % 2])
+
         def keep_mid(c, t):
             return pltpu.make_async_copy(mid.at[tile(t)], mids_h.at[c, tile(t)], mid_sem.at[t])
 
@@ -231,8 +236,9 @@
                             kept[t % 2, 0, part, cols] = silu
                             kept[t % 2, 1, part, cols] = up * (sig + silu * (1.0 - sig))
                             mid[rows, cols] = (silu * up).astype(bf16)
+                        if i % 2:
+                            keep_half(c, t, i // 2).start()
                 keep_mid(c, t).start()
-                keep(c, t).start()
 
                 @pl.when((t == 0) & (c == 0))
                 def _():
@@ -312,6 +318,12 @@
                     put_h1(t).start()
                     pl.when(t == 1)(middle)
 
+                    @pl.when(t == NT - 1)
+                    def _():
+                        arrived(J, 1)
+                        load_d(J, 0)
+
+
                     @pl.when(t > 0)
                     def _():
                         put_h1(t - 1).wait()
@@ -321,8 +333,6 @@
 
                 with jax.named_scope("fdown1"):
                     lax.fori_loop(0, NT, down, 0)
-                arrived(J, 1)
-                load_d(J, 0)
 
             return 0
 
@@ -468,7 +478,8 @@
                     do()
 
     def ready(i, m, c):
-        start, by_x_done = ((-4.3, 1.4), (-1.4, 4.9), (1.8, 8.4))[m]
+        start = 3 * m - 4.3
+        by_x_done = start + 5.7 + 0.5 * m
         after = start if i == 1 else by_x_done + (0.0, 4.0, 9.3, 14.6, 18.6)[i - 2]
         return after if c == C - 1 else after + 6.0 - 13.0 * (C - 1 - c)
 

time: 289 us -> 288 us (level)
  no operation moved by 1% of the time
where the time goes in v3:
time: 288 us
  Pallas kernels  287 us (100%)
    pallas_call x1, Pallas kernels, gradients(): pl.pallas_call(step_kernel, out_shape=[jax.ShapeDtypeStruct(*o) for o in...  272 us
    pallas_call x1, Pallas kernels, adamw(): pl.pallas_call(adamw_kernel, grid=(L, parts), out_shape=shapes, in_specs=...  14.8 us

profile of v3, /device:TPU:0, one launch (start us, length us, event | category | flops | bytes accessed | tf_op | source)
XLA Modules:
  0.0 287.8 jit_solution(14667904810213140844)
XLA Ops:
  0.6 272.1 %step.1 = (bf16[8,2,640,512]{3,2,1,0:T(8,128)(2,1)}, bf16[8,512,640]{2,1,0:T(8,128)(2,1)}, bf16[4096,640]{1,0:T(8,128)(2,1)}, bf16[4096,640]{1,0:T(8,128)(2,1)},...) custom-call(bf16[4096,640]{1,0:T(8,128)(2,1)} %bitcast.7, ...), custom_call_target="tpu_custom_call" | custom-call | flops 179999997952 | bytes 100000000 | tf_op jit(solution)/shard_map/step/pallas_call | solution.py:694
  272.8 14.8 %adamw.1 = (bf16[2,160,2048]{2,1,0:T(8,128)(2,1)}, bf16[2,160,2048]{2,1,0:T(8,128)(2,1)}, bf16[2,512,640]{2,1,0:T(8,128)(2,1)}, f32[2,160,2048]{2,1,0:T(8,128)},...) custom-call(bf16[2,4,3,4,160,128]{5,4,3,2,1,0:T(8,128)(2,1)} %bitcas, ...), custom_call_target="tpu_custom_call" | custom-call | tf_op jit(solution)/shard_map/adamw/pallas_call | solution.py:747

commit v4 on v3

--- a/solution.py
+++ b/solution.py
@@ -449,42 +449,41 @@
         put(c, m).start()
 
     SLOTS = {
-        "A0": "201",
-        "A1": "121 412 623",
-        "A2": "211",
-        "A3": "",
-        "H0": "502",
-        "H1": "301 422",
-        "H2": "100 221 512 602",
-        "H3": "311",
-        "H4": "110 401 522",
-        "H5": "321 612",
+        "A0": "121201322",
+        "A1": "412502",
+        "A2": "422602",
+        "A3": "512,100",
+        "H0": "211301623",
+        "H1": "221,311401,100",
+        "H2": "110522612,,311401",
     }
     STEPS = (None, s1, s2, s3, s4, s5, s6)
-    SLOTS = {name: [tuple(map(int, word)) for word in words.split()] for name, words in SLOTS.items()}
+
+    def events(name, layer):
+        word = (SLOTS[name].split(",") + ["", ""])[layer]
+        return [tuple(map(int, word[i : i + 3])) for i in range(0, len(word), 3)]
 
     def run(name, c):
         with jax.named_scope("slot_" + name):
-            for back in range(4):
-                todo = [(STEPS[i], m) for i, m, ago in SLOTS[name] if ago == back]
-
-                def do(todo=todo, back=back):
-                    for fn, m in todo:
-                        fn(c - back, m)
-
-                if todo and back:
-                    pl.when(c >= back)(do)
-                elif todo:
-                    do()
+            for layer, here in enumerate((c >= 0, c >= J, c < J)):
+                for back in range(4):
+                    todo = [(STEPS[i], m) for i, m, ago in events(name, layer) if ago == back]
+
+                    def do(todo=todo, back=back):
+                        for fn, m in todo:
+                            fn(c - back, m)
+
+                    if todo and (back or layer):
+                        pl.when(here & (c >= back))(do)
+                    elif todo:
+                        do()
 
     def ready(i, m, c):
-        start = 3 * m - 4.3
-        by_x_done = start + 5.7 + 0.5 * m
-        after = start if i == 1 else by_x_done + (0.0, 4.0, 9.3, 14.6, 18.6)[i - 2]
-        return after if c == C - 1 else after + 6.0 - 13.0 * (C - 1 - c)
+        after = 3.3 * m + (-4.3, 1.4, 5.4, 10.7, 16.0, 20.0)[i - 1]
+        return after - 12 * (C - 1 - c)
 
     def finish():
-        left = sorted((ready(i, m, c), i, m, c) for events in SLOTS.values() for i, m, ago in events for c in range(C - ago, C))
+        left = sorted((ready(i, m, c), i, m, c) for name in SLOTS for i, m, ago in events(name, 0) + events(name, 1) for c in range(C - ago, C))
         sent = [(path, which) for path in range(5) for which in range(2)]
         for n, (_, i, m, c) in enumerate(left):
             with jax.named_scope(f"t{i}_{m}_{c}"):
@@ -521,15 +520,13 @@
             def load_mids(chunk, t):
                 return pltpu.make_async_copy(mids_h.at[chunk - J, tile(t)], act.at[0, tile(t)], mid_sem.at[t])
 
-            def product(m, h):
-                lhs, rows = (g, a, a)[m], pl.ds(h * (N // 2), N // 2)
-                with jax.named_scope(f"dw{m}{h}"):
-                    if h == 0:
-                        half[...] = dot(lhs[rows], act[m, rows], TN)
-                    else:
-                        s0(c, m, half[...] + dot(lhs[rows], act[m, rows], TN))
-                run(f"H{2 * m + h}", c)
-                if m < h:
+            def product(m):
+                lhs, rows, more = (g, a, a)[m], pl.ds(0, N // 2), pl.ds(N // 2, N // 2)
+                with jax.named_scope(f"dw{m}"):
+                    half[...] = dot(lhs[rows], act[m, rows], TN)
+                    s0(c, m, half[...] + dot(lhs[more], act[m, more], TN))
+                run(f"H{m}", c)
+                if m == 0:
 
                     @pl.when((c >= J - 1) & (c < C - 1))
                     def _():
@@ -578,14 +575,13 @@
                     @pl.when(t == k)
                     def _(k=k):
                         run(f"A{k}", c)
-                        if k in (1, 2):
+                        if k == 1:
 
                             @pl.when(c >= J)
                             def _():
-                                if k == 1:
-                                    for t in range(NT):
-                                        load_mids(c, t).wait()
-                                product(0, k - 1)
+                                for t in range(NT):
+                                    load_mids(c, t).wait()
+                                product(0)
 
                         if k < 3:
 
@@ -629,12 +625,9 @@
                 for t in range(NT):
                     load_a0(t).wait()
 
-            for m in range(3):
-                for h in range(2):
-                    if m:
-                        product(m, h)
-                    else:
-                        pl.when(c < J)(functools.partial(product, m, h))
+            pl.when(c < J)(functools.partial(product, 0))
+            product(1)
+            product(2)
 
             def by_states(rows):
                 return dot(act[1, rows], wgu[slot, 0], TT) + dot(act[2, rows], wgu[slot, 1], TT)

time: 288 us -> 285 us (0.990)
  Pallas kernels: 287 us -> 284 us
    pallas_call x1, Pallas kernels: 272 us -> 269 us  [gradients(): pl.pallas_call(step_kernel, out_shape=[jax.ShapeDtypeStruct(*o) for o in...]
where the time goes in v4:
time: 285 us; the launch traced here: 284 us
  Pallas kernels  284 us (100%)
    pallas_call x1, Pallas kernels, gradients(): pl.pallas_call(step_kernel, out_shape=[jax.ShapeDtypeStruct(*o) for o in...  269 us
    pallas_call x1, Pallas kernels, adamw(): pl.pallas_call(adamw_kernel, grid=(L, parts), out_shape=shapes, in_specs=...  14.8 us

profile of v4, /device:TPU:0, one launch (start us, length us, event | category | flops | bytes accessed | tf_op | source)
XLA Modules:
  0.0 284.4 jit_solution(13046888732664924724)
XLA Ops:
  0.6 268.8 %step.1 = (bf16[8,2,640,512]{3,2,1,0:T(8,128)(2,1)}, bf16[8,512,640]{2,1,0:T(8,128)(2,1)}, bf16[4096,640]{1,0:T(8,128)(2,1)}, bf16[4096,640]{1,0:T(8,128)(2,1)},...) custom-call(bf16[4096,640]{1,0:T(8,128)(2,1)} %bitcast.7, ...), custom_call_target="tpu_custom_call" | custom-call | flops 179999997952 | bytes 100000000 | tf_op jit(solution)/shard_map/step/pallas_call | solution.py:687
  269.4 14.8 %adamw.1 = (bf16[2,160,2048]{2,1,0:T(8,128)(2,1)}, bf16[2,160,2048]{2,1,0:T(8,128)(2,1)}, bf16[2,512,640]{2,1,0:T(8,128)(2,1)}, f32[2,160,2048]{2,1,0:T(8,128)},...) custom-call(bf16[2,4,3,4,160,128]{5,4,3,2,1,0:T(8,128)(2,1)} %bitcas, ...), custom_call_target="tpu_custom_call" | custom-call | tf_op jit(solution)/shard_map/adamw/pallas_call | solution.py:740
